TPU v7x, 128 devices: a whole 4x4x4 slice. The times are simulated.
128 devices in a mesh: rep: 2 (over core), dp: 64 (over x, y, z).
Axes of the slice: x: 4, y: 4, z: 4, core: 2. Of those that a mesh axis runs over, the one named last changes fastest.
Arguments:
- a: bfloat16 [128, 2, 4096, 1024], P(('rep', 'dp')), parts along dimension 0
- g: bfloat16 [128, 2, 4096, 3200], P(('rep', 'dp')), parts along dimension 0
Outputs:
- output: bfloat16 [4, 1024, 3200], P('rep'), parts along dimension 0
There are 2 independent parts. A program takes and returns all parts, laid end to end along the dimension named above; each array names one.
All inputs are finite; a program needn't handle non-finite values.
Results may differ from a plain program's by a relative error of at most 0.012.
Values are sent between devices in bfloat16 or wider.
A program may use at most 1.5 GiB of HBM per device.

v0:
```python
import jax
import jax.numpy as jnp


def solution(mesh):
    groups = mesh.shape["rep"]

    def step(a, g):
        a, g = (t.reshape(groups, -1, *t.shape[1:]) for t in (a, g))
        sums = jnp.einsum("rsntd,rsntf->rndf", a, g, preferred_element_type=jnp.float32)
        return sums.astype(jnp.bfloat16).reshape(-1, *sums.shape[2:])

    return step
```

profile of v0, /device:TPU:0, one launch (start us, length us, event | category | flops | bytes accessed | tf_op | source)
XLA Modules:
  0.0 653.4 jit_solution(9874151454964867488)
XLA Ops:
  0.0 67.8 %fusion.3 = f32[1,2,1024,3200]{3,2,1,0:T(8,128)} fusion(bf16[1,2,4096,3200]{3,2,1,0:T(8,128)(2,1)} %param.1, bf16[1,2,4096,1024]{3,2,1,0:T(8,128)(2,1)} %param), kind=kOutput, calls=%fused_computation.4 | convolution fusion | flops 53687091200 | bytes 95420416 | tf_op jit(solution)/rsntd,rsntf->rndf/dot_general | solution.py:10
  67.8 585.6 %all-reduce.2 = bf16[1,2,1024,3200]{3,2,1,0:T(8,128)(2,1)} all-reduce(f32[1,2,1024,3200]{3,2,1,0:T(8,128)} %fusion.3), channel_id=1, replica_groups=[2,64]<=[128], use_global_device_ids=true, to_apply=%add.clone | all-reduce | flops 6553600 | bytes 39321600 | tf_op jit(solution)/rsntd,rsntf->rndf/dot_general | solution.py:10
where the time goes:
time: 654 us; the launch traced here: 653 us
  blocking collectives  586 us (90%)
  matrix products  67.8 us (10%)
    dot_general x1, blocking collectives, step(): jnp.einsum('rsntd,rsntf->rndf', a, g, preferred_element_type=jnp.float32)  586 us
    dot_general x1, matrix products, step(): jnp.einsum('rsntd,rsntf->rndf', a, g, preferred_element_type=jnp.float32)  67.8 us

commit v1 on v0

v1 whole, which is shorter than its diff:
```python
import functools

import jax
import jax.numpy as jnp
from jax import lax
from jax.experimental import pallas as pl
from jax.experimental.pallas import tpu as pltpu
from jax.sharding import PartitionSpec as P

MESH = pl.DeviceIdType.MESH
BF, F32 = jnp.bfloat16, jnp.float32

D, FF, TOKENS = 1024, 3200, 4096
COLS = 256
PER = FF // COLS
ITEMS = 2 * PER + 1
MIXED = PER
KB = 1024
LAGS = (0, 2, 4, 5, 7, 8, 9, 10, 12, 14, 16)
SLOTS = LAGS[10] + 1
FSLOTS = 8


def kernel(a_hbm, g_hbm, out, a_buf, g_buf, acc, terms, r1, c1, f1, s2, r2, f2, s3, r3,
           a_sem, g_sem, send, opp1, rest1, opp2, rest2, in3, ag3, fwd2, ag2, fwd1, ag1):
    dp = lax.axis_index("dp")
    x, y, z = dp // 16, (dp // 4) % 4, dp % 4

    def axis(k):
        w0, w1, w2 = (1 - k) * (2 - k) // 2, k * (2 - k), k * (k - 1) // 2
        c, s = x * w0 + y * w1 + z * w2, 16 * w0 + 4 * w1 + w2
        return c, lambda d: dp + s * ((c + d) % 4 - c)

    def rows(start, size):
        return pl.ds(pl.multiple_of(start, 16), size)

    def a_copy(n, j):
        return pltpu.make_async_copy(a_hbm.at[0, n, pl.ds(j * KB, KB), :], a_buf.at[pl.ds(j * KB, KB), :], a_sem.at[j])

    def g_copy(n, first, width, slot, at):
        return pltpu.make_async_copy(
            g_hbm.at[0, n, :, pl.ds(first, width)], g_buf.at[slot, :, pl.ds(at, width)], g_sem.at[slot])

    def g_start(t):
        @pl.when((t < MIXED) | ((t > MIXED) & (t < ITEMS)))
        def _():
            n = t // (MIXED + 1)
            b = t - n * (MIXED + 1)
            g_copy(n, pl.multiple_of(b * COLS, COLS), COLS, t % 2, 0).start()

        @pl.when(t == MIXED)
        def _():
            g_copy(0, PER * COLS, 128, MIXED % 2, 0).start()
            g_copy(1, PER * COLS, 128, MIXED % 2, 128).start()

    def g_wait(t):
        g_copy(0, 0, COLS, t % 2, 0).wait()

    def dot(a, g):
        return lax.dot_general(a, g, (((0,), (0,)), ((), ())), preferred_element_type=F32)

    def blocked(slot, cols, row0, before, after):
        for j in range(TOKENS // KB):
            before(j)
            part = dot(a_buf[pl.ds(j * KB, KB), :], g_buf[slot, pl.ds(j * KB, KB), cols])
            if j == 0:
                acc[:, cols] = part
            else:
                acc[:, cols] += part
            after(j)
        terms[pl.ds(row0, D), cols] = acc[:, cols].astype(BF)

    def push(i, src, dst, sem, to):
        pltpu.make_async_remote_copy(
            src_ref=src, dst_ref=dst, send_sem=send.at[i % SLOTS], recv_sem=sem,
            device_id={"dp": to}, device_id_type=MESH).start()

    def arrived(ref, sem):
        pltpu.make_async_copy(ref, ref, sem).wait()

    def place(i):
        k = i % 3
        return axis(k), axis((k + 1) % 3), axis((k + 2) % 3)

    def up(ref):
        return ref[...].astype(F32)

    def e0(i):
        (c, to), _, _ = place(i)
        base = i * D
        q = lambda d, h: rows(base + 256 * ((c + d) % 4) + 128 * h, 128)
        push(i, terms.at[q(2, 0)], r1.at[i, 0, pl.ds(0, 128)], opp1.at[i, 0], to(1))
        push(i, terms.at[q(2, 1)], r1.at[i, 1, pl.ds(0, 128)], opp1.at[i, 1], to(3))
        push(i, terms.at[q(1, 1)], r1.at[i, 0, pl.ds(256, 128)], rest1.at[i, 0], to(1))
        push(i, terms.at[q(3, 0)], r1.at[i, 1, pl.ds(128, 128)], rest1.at[i, 1], to(3))

    def e1(i):
        (c, to), _, _ = place(i)
        base, s = i * D, i % SLOTS
        for side, (d, h) in enumerate(((1, 0), (3, 1))):
            arrived(r1.at[i, side, pl.ds(0, 128)], opp1.at[i, side])
            own = terms[rows(base + 256 * ((c + d) % 4) + 128 * h, 128), :].astype(F32)
            c1[s, side] = (own + r1[i, side, pl.ds(0, 128)].astype(F32)).astype(BF)
            push(i, c1.at[s, side], r1.at[i, side, pl.ds(128 + 128 * h, 128)], rest1.at[i, side], to(d))

    def e2(i):
        (c, _), (d2, to), _ = place(i)
        base, s, f = i * D, i % SLOTS, i % FSLOTS
        for side in range(2):
            arrived(r1.at[i, side, pl.ds(128, 256)], rest1.at[i, side])
        f1[f] = (terms[rows(base + 256 * c, 256), :].astype(F32)
                 + r1[i, 0, pl.ds(128, 256)].astype(F32) + r1[i, 1, pl.ds(128, 256)].astype(F32))
        s2[s, pl.ds(0, 64)] = f1[f, rows(64 * ((d2 + 2) % 4), 64)].astype(BF)
        s2[s, pl.ds(64, 32)] = f1[f, rows(64 * ((d2 + 1) % 4) + 32, 32)].astype(BF)
        s2[s, pl.ds(96, 32)] = f1[f, rows(64 * ((d2 + 3) % 4), 32)].astype(BF)
        push(i, s2.at[s, pl.ds(0, 32)], r2.at[i, 0, pl.ds(0, 32)], opp2.at[i, 0], to(1))
        push(i, s2.at[s, pl.ds(32, 32)], r2.at[i, 1, pl.ds(0, 32)], opp2.at[i, 1], to(3))
        push(i, s2.at[s, pl.ds(64, 32)], r2.at[i, 0, pl.ds(64, 32)], rest2.at[i, 0], to(1))
        push(i, s2.at[s, pl.ds(96, 32)], r2.at[i, 1, pl.ds(32, 32)], rest2.at[i, 1], to(3))

    def e3(i):
        _, (c, to), _ = place(i)
        s, f = i % SLOTS, i % FSLOTS
        for side, (d, h) in enumerate(((1, 0), (3, 1))):
            arrived(r2.at[i, side, pl.ds(0, 32)], opp2.at[i, side])
            own = f1[f, rows(64 * ((c + d) % 4) + 32 * h, 32)]
            s2[s, pl.ds(128 + 32 * side, 32)] = (own + r2[i, side, pl.ds(0, 32)].astype(F32)).astype(BF)
            push(i, s2.at[s, pl.ds(128 + 32 * side, 32)], r2.at[i, side, pl.ds(32 + 32 * h, 32)],
                 rest2.at[i, side], to(d))

    def e4(i):
        _, (c, _), (d3, to) = place(i)
        s, f = i % SLOTS, i % FSLOTS
        for side in range(2):
            arrived(r2.at[i, side, pl.ds(32, 64)], rest2.at[i, side])
        f2[f] = (f1[f, rows(64 * c, 64)]
                 + r2[i, 0, pl.ds(32, 64)].astype(F32) + r2[i, 1, pl.ds(32, 64)].astype(F32))
        for d in (2, 1, 3):
            s3[s, pl.ds(16 * (d - 1), 16)] = f2[f, rows(16 * ((d3 + d) % 4), 16)].astype(BF)
            push(i, s3.at[s, pl.ds(16 * (d - 1), 16)], r3.at[i, pl.ds(16 * (d - 1), 16)], in3.at[i], to(d))

    def e5(i):
        (p1, _), (p2, _), (p3, to) = place(i)
        f = i % FSLOTS
        arrived(r3.at[i], in3.at[i])
        total = f2[f, rows(16 * p3, 16)]
        for d in range(3):
            total += r3[i, pl.ds(16 * d, 16)].astype(F32)
        mine = rows(i * D + 256 * p1 + 64 * p2 + 16 * p3, 16)
        out[mine, :] = total.astype(BF)
        for d in (2, 1, 3):
            push(i, out.at[mine], out.at[mine], ag3.at[i], to(d))

    def gather(i, base, size, c, to, fwd, rest):
        half = size // 2
        h0, h1 = (out.at[rows(base + size * c + half * h, half)] for h in range(2))
        push(i, h0, h0, fwd.at[i, 0], to(1))
        push(i, h1, h1, fwd.at[i, 1], to(3))
        push(i, h1, h1, rest.at[i, 0], to(1))
        push(i, h0, h0, rest.at[i, 1], to(3))

    def onward(i, base, size, c, to, fwd, rest):
        half = size // 2
        for side, (d, h) in enumerate(((1, 0), (3, 1))):
            ref = out.at[rows(base + size * ((c - d) % 4) + half * h, half)]
            arrived(ref, fwd.at[i, side])
            push(i, ref, ref, rest.at[i, side], to(d))

    def e6(i):
        (p1, _), (p2, to), _ = place(i)
        arrived(out.at[pl.ds(0, 48)], ag3.at[i])
        gather(i, i * D + 256 * p1, 64, p2, to, fwd2, ag2)

    def e7(i):
        (p1, _), (p2, to), _ = place(i)
        onward(i, i * D + 256 * p1, 64, p2, to, fwd2, ag2)

    def e8(i):
        (p1, to), _, _ = place(i)
        for side in range(2):
            arrived(out.at[pl.ds(0, 64)], ag2.at[i, side])
        gather(i, i * D, 256, p1, to, fwd1, ag1)

    def e9(i):
        (p1, to), _, _ = place(i)
        onward(i, i * D, 256, p1, to, fwd1, ag1)

    def e10(i):
        for side in range(2):
            arrived(out.at[pl.ds(0, 256)], ag1.at[i, side])
        arrived(terms.at[pl.ds(0, 4 * 512 - 32)], send.at[i % SLOTS])

    events = (e0, e1, e2, e3, e4, e5, e6, e7, e8, e9, e10)

    g_start(0)
    for j in range(TOKENS // KB):
        a_copy(0, j).start()
    barrier = pltpu.get_barrier_semaphore()
    for k in range(3):
        _, to = axis(k)
        for d in range(1, 4):
            pl.semaphore_signal(barrier, inc=1, device_id={"dp": to(d)}, device_id_type=MESH)
    pl.semaphore_wait(barrier, 9)

    def slot(t, carry):
        g_start(t + 1)

        @pl.when(t < ITEMS)
        def _():
            g_wait(t)

        @pl.when(t == 0)
        def _():
            blocked(0, slice(None), 0, lambda j: a_copy(0, j).wait(), lambda j: None)

        @pl.when(t == MIXED)
        def _():
            blocked(MIXED % 2, slice(0, 128), MIXED * D, lambda j: None, lambda j: a_copy(1, j).start())
            blocked(MIXED % 2, slice(128, 256), MIXED * D, lambda j: a_copy(1, j).wait(), lambda j: None)

        @pl.when((t > 0) & (t < ITEMS) & (t != MIXED))
        def _():
            terms[rows(t * D, D), :] = dot(a_buf[...], g_buf[t % 2]).astype(BF)

        for lag, event in zip(LAGS, events):
            i = t - lag

            @pl.when((i >= 0) & (i < ITEMS))
            def _():
                event(i)

        return carry

    lax.fori_loop(0, ITEMS + LAGS[10], slot, 0)


def spread(src, dst, sem):
    copies = []
    for i in range(ITEMS):
        if i == MIXED:
            for n in range(2):
                copies.append((src.at[pl.ds(i * D, D), pl.ds(128 * n, 128)], dst.at[n, :, pl.ds(PER * COLS, 128)]))
        else:
            n = i // (MIXED + 1)
            b = i - n * (MIXED + 1)
            copies.append((src.at[pl.ds(i * D, D), :], dst.at[n, :, pl.ds(b * COLS, COLS)]))
    copies = [pltpu.make_async_copy(s, d, sem.at[j]) for j, (s, d) in enumerate(copies)]
    for c in copies:
        c.start()
    for c in copies:
        c.wait()


def solution(mesh):
    def step(a, g):
        dma = pltpu.SemaphoreType.DMA
        sums = pl.pallas_call(
            kernel,
            out_shape=pltpu.VMEM((ITEMS * D, COLS), BF),
            in_specs=[pl.BlockSpec(memory_space=pltpu.HBM)] * 2,
            out_specs=pl.BlockSpec(memory_space=pltpu.VMEM),
            scratch_shapes=[
                pltpu.VMEM((TOKENS, D), BF),
                pltpu.VMEM((2, TOKENS, COLS), BF),
                pltpu.VMEM((D, COLS), F32),
                pltpu.VMEM((ITEMS * D, COLS), BF),
                pltpu.VMEM((ITEMS, 2, 384, COLS), BF),
                pltpu.VMEM((SLOTS, 2, 128, COLS), BF),
                pltpu.VMEM((FSLOTS, 256, COLS), F32),
                pltpu.VMEM((SLOTS, 192, COLS), BF),
                pltpu.VMEM((ITEMS, 2, 96, COLS), BF),
                pltpu.VMEM((FSLOTS, 64, COLS), F32),
                pltpu.VMEM((SLOTS, 48, COLS), BF),
                pltpu.VMEM((ITEMS, 48, COLS), BF),
                dma((TOKENS // KB,)),
                dma((2,)),
                dma((SLOTS,)),
                dma((ITEMS, 2)),
                dma((ITEMS, 2)),
                dma((ITEMS, 2)),
                dma((ITEMS, 2)),
                dma((ITEMS,)),
                dma((ITEMS,)),
                dma((ITEMS, 2)),
                dma((ITEMS, 2)),
                dma((ITEMS, 2)),
                dma((ITEMS, 2)),
            ],
            compiler_params=pltpu.CompilerParams(
                collective_id=0, has_side_effects=True, vmem_limit_bytes=50 * 2**20),
        )(a, g)
        return pl.pallas_call(
            spread,
            out_shape=jax.ShapeDtypeStruct((2, D, FF), BF),
            in_specs=[pl.BlockSpec(memory_space=pltpu.VMEM)],
            out_specs=pl.BlockSpec(memory_space=pltpu.HBM),
            scratch_shapes=[dma((ITEMS + 1,))],
            compiler_params=pltpu.CompilerParams(vmem_limit_bytes=2 * 2**20),
        )(sums)

    return jax.shard_map(
        step, mesh=mesh, in_specs=(P(("rep", "dp")), P(("rep", "dp"))), out_specs=P("rep"), check_vma=False)
```

time: 654 us -> 164 us (0.25)
  blocking collectives: 586 us -> 0 us
  Pallas kernels: 0 us -> 163 us
  matrix products: 67.8 us -> 0 us
    dot_general x1 -> x0, blocking collectives: 586 us -> none  [step(): jnp.einsum('rsntd,rsntf->rndf', a, g, preferred_element_type=jnp.float32)]
    pallas_call x0 -> x2, Pallas kernels: none -> 163 us  [the longest x1 159 us: step(): pl.pallas_call(kernel, out_shape=pltpu.VMEM((ITEMS * D, COLS), BF), in_sp...]
    dot_general x1 -> x0, matrix products: 67.8 us -> none  [step(): jnp.einsum('rsntd,rsntf->rndf', a, g, preferred_element_type=jnp.float32)]
where the time goes in v1:
time: 164 us
  Pallas kernels  163 us (99%)
    pallas_call x1, Pallas kernels, step(): pl.pallas_call(kernel, out_shape=pltpu.VMEM((ITEMS * D, COLS), BF), in_sp...  159 us
    pallas_call x1, Pallas kernels, step(): pl.pallas_call(spread, out_shape=jax.ShapeDtypeStruct((2, D, FF), BF), in...  4.92 us

profile of v1, /device:TPU:0, one launch (start us, length us, event | category | flops | bytes accessed | tf_op | source)
XLA Modules:
  0.0 163.5 jit_solution(849442741921875748)
XLA Ops:
  0.0 158.6 %shard_map.28.src = bf16[25600,256]{1,0:T(8,128)(2,1)S(1)} custom-call(bf16[1,2,4096,1024]{3,2,1,0:T(8,128)(2,1)} %a_hbm.1, bf16[1,2,4096,3200]{3,2,1,0:T(8,128)(2,1)} %g_hbm.1), custom_call_target="tpu_custom_call" | custom-call | tf_op jit(solution)/shard_map/pallas_call | solution.py:257
  158.6 4.9 %shard_map.29 = bf16[2,1024,3200]{2,1,0:T(8,128)(2,1)} custom-call(bf16[25600,256]{1,0:T(8,128)(2,1)S(1)} %shard_map.28.src), custom_call_target="tpu_custom_call" | custom-call | tf_op jit(solution)/shard_map/pallas_call | solution.py:292

commit v2 on v1

--- a/solution.py
+++ b/solution.py
@@ -16,20 +16,25 @@
 ITEMS = 2 * PER + 1
 MIXED = PER
 KB = 1024
-LAGS = (0, 2, 4, 5, 7, 8, 9, 10, 12, 14, 16)
-SLOTS = LAGS[10] + 1
+LAGS = (0, 2, 4, 5, 7, 9, 11, 13, 16, 26, 39, 0, 16)
+ORDER = (2, 4, 5, 0, 11, 10, 7, 6, 1, 9, 3, 8, 12)
+SLOTS = ITEMS
 FSLOTS = 8
 
 
 def kernel(a_hbm, g_hbm, out, a_buf, g_buf, acc, terms, r1, c1, f1, s2, r2, f2, s3, r3,
            a_sem, g_sem, send, opp1, rest1, opp2, rest2, in3, ag3, fwd2, ag2, fwd1, ag1):
-    dp = lax.axis_index("dp")
+    dp, rep = lax.axis_index("dp"), lax.axis_index("rep")
     x, y, z = dp // 16, (dp // 4) % 4, dp % 4
 
-    def axis(k):
+    def axis(n):
+        k = (n + rep) % 3
         w0, w1, w2 = (1 - k) * (2 - k) // 2, k * (2 - k), k * (k - 1) // 2
         c, s = x * w0 + y * w1 + z * w2, 16 * w0 + 4 * w1 + w2
-        return c, lambda d: dp + s * ((c + d) % 4 - c)
+        ids = [dp + s * ((c + d) % 4 - c) for d in range(4)]
+        return c, lambda d: ids[d]
+
+    axes = [axis(n) for n in range(3)]
 
     def rows(start, size):
         return pl.ds(pl.multiple_of(start, 16), size)
@@ -72,40 +77,41 @@
 
     def push(i, src, dst, sem, to):
         pltpu.make_async_remote_copy(
-            src_ref=src, dst_ref=dst, send_sem=send.at[i % SLOTS], recv_sem=sem,
+            src_ref=src, dst_ref=dst, send_sem=send.at[i], recv_sem=sem,
             device_id={"dp": to}, device_id_type=MESH).start()
 
     def arrived(ref, sem):
         pltpu.make_async_copy(ref, ref, sem).wait()
 
-    def place(i):
-        k = i % 3
-        return axis(k), axis((k + 1) % 3), axis((k + 2) % 3)
-
-    def up(ref):
-        return ref[...].astype(F32)
-
-    def e0(i):
-        (c, to), _, _ = place(i)
+    def place(k):
+        return axes[k], axes[(k + 1) % 3], axes[(k + 2) % 3]
+
+    def e0(i, k):
+        (c, to), _, _ = place(k)
         base = i * D
         q = lambda d, h: rows(base + 256 * ((c + d) % 4) + 128 * h, 128)
         push(i, terms.at[q(2, 0)], r1.at[i, 0, pl.ds(0, 128)], opp1.at[i, 0], to(1))
         push(i, terms.at[q(2, 1)], r1.at[i, 1, pl.ds(0, 128)], opp1.at[i, 1], to(3))
+
+    def e11(i, k):
+        (c, to), _, _ = place(k)
+        base = i * D
+        q = lambda d, h: rows(base + 256 * ((c + d) % 4) + 128 * h, 128)
         push(i, terms.at[q(1, 1)], r1.at[i, 0, pl.ds(256, 128)], rest1.at[i, 0], to(1))
         push(i, terms.at[q(3, 0)], r1.at[i, 1, pl.ds(128, 128)], rest1.at[i, 1], to(3))
 
-    def e1(i):
-        (c, to), _, _ = place(i)
-        base, s = i * D, i % SLOTS
+    def e1(i, k):
+        (c, to), _, _ = place(k)
+        base, s = i * D, i
         for side, (d, h) in enumerate(((1, 0), (3, 1))):
             arrived(r1.at[i, side, pl.ds(0, 128)], opp1.at[i, side])
             own = terms[rows(base + 256 * ((c + d) % 4) + 128 * h, 128), :].astype(F32)
             c1[s, side] = (own + r1[i, side, pl.ds(0, 128)].astype(F32)).astype(BF)
             push(i, c1.at[s, side], r1.at[i, side, pl.ds(128 + 128 * h, 128)], rest1.at[i, side], to(d))
 
-    def e2(i):
-        (c, _), (d2, to), _ = place(i)
-        base, s, f = i * D, i % SLOTS, i % FSLOTS
+    def e2(i, k):
+        (c, _), (d2, to), _ = place(k)
+        base, s, f = i * D, i, i % FSLOTS
         for side in range(2):
             arrived(r1.at[i, side, pl.ds(128, 256)], rest1.at[i, side])
         f1[f] = (terms[rows(base + 256 * c, 256), :].astype(F32)
@@ -118,9 +124,9 @@
         push(i, s2.at[s, pl.ds(64, 32)], r2.at[i, 0, pl.ds(64, 32)], rest2.at[i, 0], to(1))
         push(i, s2.at[s, pl.ds(96, 32)], r2.at[i, 1, pl.ds(32, 32)], rest2.at[i, 1], to(3))
 
-    def e3(i):
-        _, (c, to), _ = place(i)
-        s, f = i % SLOTS, i % FSLOTS
+    def e3(i, k):
+        _, (c, to), _ = place(k)
+        s, f = i, i % FSLOTS
         for side, (d, h) in enumerate(((1, 0), (3, 1))):
             arrived(r2.at[i, side, pl.ds(0, 32)], opp2.at[i, side])
             own = f1[f, rows(64 * ((c + d) % 4) + 32 * h, 32)]
@@ -128,9 +134,9 @@
             push(i, s2.at[s, pl.ds(128 + 32 * side, 32)], r2.at[i, side, pl.ds(32 + 32 * h, 32)],
                  rest2.at[i, side], to(d))
 
-    def e4(i):
-        _, (c, _), (d3, to) = place(i)
-        s, f = i % SLOTS, i % FSLOTS
+    def e4(i, k):
+        _, (c, _), (d3, to) = place(k)
+        s, f = i, i % FSLOTS
         for side in range(2):
             arrived(r2.at[i, side, pl.ds(32, 64)], rest2.at[i, side])
         f2[f] = (f1[f, rows(64 * c, 64)]
@@ -139,8 +145,8 @@
             s3[s, pl.ds(16 * (d - 1), 16)] = f2[f, rows(16 * ((d3 + d) % 4), 16)].astype(BF)
             push(i, s3.at[s, pl.ds(16 * (d - 1), 16)], r3.at[i, pl.ds(16 * (d - 1), 16)], in3.at[i], to(d))
 
-    def e5(i):
-        (p1, _), (p2, _), (p3, to) = place(i)
+    def e5(i, k):
+        (p1, _), (p2, _), (p3, to) = place(k)
         f = i % FSLOTS
         arrived(r3.at[i], in3.at[i])
         total = f2[f, rows(16 * p3, 16)]
@@ -151,11 +157,17 @@
         for d in (2, 1, 3):
             push(i, out.at[mine], out.at[mine], ag3.at[i], to(d))
 
-    def gather(i, base, size, c, to, fwd, rest):
+    def halves(base, size, c):
         half = size // 2
-        h0, h1 = (out.at[rows(base + size * c + half * h, half)] for h in range(2))
+        return [out.at[rows(base + size * c + half * h, half)] for h in range(2)]
+
+    def gather(i, base, size, c, to, fwd):
+        h0, h1 = halves(base, size, c)
         push(i, h0, h0, fwd.at[i, 0], to(1))
         push(i, h1, h1, fwd.at[i, 1], to(3))
+
+    def others(i, base, size, c, to, rest):
+        h0, h1 = halves(base, size, c)
         push(i, h1, h1, rest.at[i, 0], to(1))
         push(i, h0, h0, rest.at[i, 1], to(3))
 
@@ -166,72 +178,82 @@
             arrived(ref, fwd.at[i, side])
             push(i, ref, ref, rest.at[i, side], to(d))
 
-    def e6(i):
-        (p1, _), (p2, to), _ = place(i)
+    def e6(i, k):
+        (p1, _), (p2, to), _ = place(k)
         arrived(out.at[pl.ds(0, 48)], ag3.at[i])
-        gather(i, i * D + 256 * p1, 64, p2, to, fwd2, ag2)
-
-    def e7(i):
-        (p1, _), (p2, to), _ = place(i)
+        gather(i, i * D + 256 * p1, 64, p2, to, fwd2)
+        others(i, i * D + 256 * p1, 64, p2, to, ag2)
+
+    def e7(i, k):
+        (p1, _), (p2, to), _ = place(k)
         onward(i, i * D + 256 * p1, 64, p2, to, fwd2, ag2)
 
-    def e8(i):
-        (p1, to), _, _ = place(i)
+    def e8(i, k):
+        (p1, to), _, _ = place(k)
         for side in range(2):
             arrived(out.at[pl.ds(0, 64)], ag2.at[i, side])
-        gather(i, i * D, 256, p1, to, fwd1, ag1)
-
-    def e9(i):
-        (p1, to), _, _ = place(i)
+        gather(i, i * D, 256, p1, to, fwd1)
+
+    def e12(i, k):
+        (p1, to), _, _ = place(k)
+        others(i, i * D, 256, p1, to, ag1)
+
+    def e9(i, k):
+        (p1, to), _, _ = place(k)
         onward(i, i * D, 256, p1, to, fwd1, ag1)
 
-    def e10(i):
+    def e10(i, k):
         for side in range(2):
             arrived(out.at[pl.ds(0, 256)], ag1.at[i, side])
-        arrived(terms.at[pl.ds(0, 4 * 512 - 32)], send.at[i % SLOTS])
-
-    events = (e0, e1, e2, e3, e4, e5, e6, e7, e8, e9, e10)
+        arrived(terms.at[pl.ds(0, 4 * 512 - 32)], send.at[i])
+
+    events = (e0, e1, e2, e3, e4, e5, e6, e7, e8, e9, e10, e11, e12)
 
     g_start(0)
     for j in range(TOKENS // KB):
         a_copy(0, j).start()
+    g_start(1)
     barrier = pltpu.get_barrier_semaphore()
     for k in range(3):
-        _, to = axis(k)
+        _, to = axes[k]
         for d in range(1, 4):
             pl.semaphore_signal(barrier, inc=1, device_id={"dp": to(d)}, device_id_type=MESH)
+    g_wait(0)
+    blocked(0, slice(None), 0, lambda j: a_copy(0, j).wait(), lambda j: None)
     pl.semaphore_wait(barrier, 9)
 
-    def slot(t, carry):
-        g_start(t + 1)
-
-        @pl.when(t < ITEMS)
+    def multiply(t, first):
+        @pl.when(t > 0)
+        def _():
+            g_start(t + 1)
+
+        @pl.when((t > 0) & (t < ITEMS))
         def _():
             g_wait(t)
 
-        @pl.when(t == 0)
-        def _():
-            blocked(0, slice(None), 0, lambda j: a_copy(0, j).wait(), lambda j: None)
-
-        @pl.when(t == MIXED)
-        def _():
-            blocked(MIXED % 2, slice(0, 128), MIXED * D, lambda j: None, lambda j: a_copy(1, j).start())
-            blocked(MIXED % 2, slice(128, 256), MIXED * D, lambda j: a_copy(1, j).wait(), lambda j: None)
-
-        @pl.when((t > 0) & (t < ITEMS) & (t != MIXED))
+        if first:
+            @pl.when(t == MIXED)
+            def _():
+                blocked(MIXED % 2, slice(0, 128), MIXED * D, lambda j: None, lambda j: a_copy(1, j).start())
+                blocked(MIXED % 2, slice(128, 256), MIXED * D, lambda j: a_copy(1, j).wait(), lambda j: None)
+
+        @pl.when(((t > 0) & (t < ITEMS) & (t != MIXED)) if first else t < ITEMS)
         def _():
             terms[rows(t * D, D), :] = dot(a_buf[...], g_buf[t % 2]).astype(BF)
 
-        for lag, event in zip(LAGS, events):
-            i = t - lag
-
-            @pl.when((i >= 0) & (i < ITEMS))
-            def _():
-                event(i)
+    def around(r, carry):
+        for c in range(3):
+            multiply(3 * r + c, c == 0)
+            for e in ORDER:
+                i = 3 * r + c - LAGS[e]
+
+                @pl.when((i >= 0) & (i < ITEMS))
+                def _():
+                    events[e](i, (c - LAGS[e]) % 3)
 
         return carry
 
-    lax.fori_loop(0, ITEMS + LAGS[10], slot, 0)
+    lax.fori_loop(0, (ITEMS + LAGS[10] + 2) // 3, around, 0)
 
 
 def spread(src, dst, sem):
@@ -287,7 +309,7 @@
                 dma((ITEMS, 2)),
             ],
             compiler_params=pltpu.CompilerParams(
-                collective_id=0, has_side_effects=True, vmem_limit_bytes=50 * 2**20),
+                collective_id=0, has_side_effects=True, vmem_limit_bytes=51 * 2**20),
         )(a, g)
         return pl.pallas_call(
             spread,

time: 164 us -> 145 us (0.88)
  Pallas kernels: 163 us -> 144 us
    pallas_call x1, Pallas kernels: 159 us -> 140 us  [step(): pl.pallas_call(kernel, out_shape=pltpu.VMEM((ITEMS * D, COLS), BF), in_sp...]
where the time goes in v2:
time: 145 us
  Pallas kernels  144 us (99%)
    pallas_call x1, Pallas kernels, step(): pl.pallas_call(kernel, out_shape=pltpu.VMEM((ITEMS * D, COLS), BF), in_sp...  140 us
    pallas_call x1, Pallas kernels, step(): pl.pallas_call(spread, out_shape=jax.ShapeDtypeStruct((2, D, FF), BF), in...  4.92 us

profile of v2, /device:TPU:0, one launch (start us, length us, event | category | flops | bytes accessed | tf_op | source)
XLA Modules:
  0.0 144.6 jit_solution(11407816411558795234)
XLA Ops:
  0.0 139.5 %shard_map.28.src = bf16[25600,256]{1,0:T(8,128)(2,1)S(1)} custom-call(bf16[1,2,4096,1024]{3,2,1,0:T(8,128)(2,1)} %a_hbm.1, bf16[1,2,4096,3200]{3,2,1,0:T(8,128)(2,1)} %g_hbm.1), custom_call_target="tpu_custom_call" | custom-call | tf_op jit(solution)/shard_map/pallas_call | solution.py:279
  139.5 4.9 %shard_map.29 = bf16[2,1024,3200]{2,1,0:T(8,128)(2,1)} custom-call(bf16[25600,256]{1,0:T(8,128)(2,1)S(1)} %shard_map.28.src), custom_call_target="tpu_custom_call" | custom-call | tf_op jit(solution)/shard_map/pallas_call | solution.py:314

commit v3 on v2

--- a/solution.py
+++ b/solution.py
@@ -15,15 +15,15 @@
 PER = FF // COLS
 ITEMS = 2 * PER + 1
 MIXED = PER
-KB = 1024
-LAGS = (0, 2, 4, 5, 7, 9, 11, 13, 16, 26, 39, 0, 16)
-ORDER = (2, 4, 5, 0, 11, 10, 7, 6, 1, 9, 3, 8, 12)
+KB = 2048
+LAGS = (0, 2, 4, 0, 7, 9, 11, 0, 14, 27, 41, 0, 14)
+ORDER = (2, 4, 5, 0, 11, 10, 6, 1, 9, 8, 12)
 SLOTS = ITEMS
 FSLOTS = 8
 
 
 def kernel(a_hbm, g_hbm, out, a_buf, g_buf, acc, terms, r1, c1, f1, s2, r2, f2, s3, r3,
-           a_sem, g_sem, send, opp1, rest1, opp2, rest2, in3, ag3, fwd2, ag2, fwd1, ag1):
+           a_sem, g_sem, send, opp1, rest1, in2, in3, ag3, ag2, fwd1, ag1):
     dp, rep = lax.axis_index("dp"), lax.axis_index("rep")
     x, y, z = dp // 16, (dp // 4) % 4, dp % 4
 
@@ -116,31 +116,19 @@
             arrived(r1.at[i, side, pl.ds(128, 256)], rest1.at[i, side])
         f1[f] = (terms[rows(base + 256 * c, 256), :].astype(F32)
                  + r1[i, 0, pl.ds(128, 256)].astype(F32) + r1[i, 1, pl.ds(128, 256)].astype(F32))
-        s2[s, pl.ds(0, 64)] = f1[f, rows(64 * ((d2 + 2) % 4), 64)].astype(BF)
-        s2[s, pl.ds(64, 32)] = f1[f, rows(64 * ((d2 + 1) % 4) + 32, 32)].astype(BF)
-        s2[s, pl.ds(96, 32)] = f1[f, rows(64 * ((d2 + 3) % 4), 32)].astype(BF)
-        push(i, s2.at[s, pl.ds(0, 32)], r2.at[i, 0, pl.ds(0, 32)], opp2.at[i, 0], to(1))
-        push(i, s2.at[s, pl.ds(32, 32)], r2.at[i, 1, pl.ds(0, 32)], opp2.at[i, 1], to(3))
-        push(i, s2.at[s, pl.ds(64, 32)], r2.at[i, 0, pl.ds(64, 32)], rest2.at[i, 0], to(1))
-        push(i, s2.at[s, pl.ds(96, 32)], r2.at[i, 1, pl.ds(32, 32)], rest2.at[i, 1], to(3))
-
-    def e3(i, k):
-        _, (c, to), _ = place(k)
-        s, f = i, i % FSLOTS
-        for side, (d, h) in enumerate(((1, 0), (3, 1))):
-            arrived(r2.at[i, side, pl.ds(0, 32)], opp2.at[i, side])
-            own = f1[f, rows(64 * ((c + d) % 4) + 32 * h, 32)]
-            s2[s, pl.ds(128 + 32 * side, 32)] = (own + r2[i, side, pl.ds(0, 32)].astype(F32)).astype(BF)
-            push(i, s2.at[s, pl.ds(128 + 32 * side, 32)], r2.at[i, side, pl.ds(32 + 32 * h, 32)],
-                 rest2.at[i, side], to(d))
+        for d in (2, 1, 3):
+            piece = pl.ds(64 * (d - 1), 64)
+            s2[s, piece] = f1[f, rows(64 * ((d2 + d) % 4), 64)].astype(BF)
+            push(i, s2.at[s, piece], r2.at[i, piece], in2.at[i], to(d))
 
     def e4(i, k):
         _, (c, _), (d3, to) = place(k)
         s, f = i, i % FSLOTS
-        for side in range(2):
-            arrived(r2.at[i, side, pl.ds(32, 64)], rest2.at[i, side])
-        f2[f] = (f1[f, rows(64 * c, 64)]
-                 + r2[i, 0, pl.ds(32, 64)].astype(F32) + r2[i, 1, pl.ds(32, 64)].astype(F32))
+        arrived(r2.at[i], in2.at[i])
+        total = f1[f, rows(64 * c, 64)]
+        for d in range(3):
+            total += r2[i, pl.ds(64 * d, 64)].astype(F32)
+        f2[f] = total
         for d in (2, 1, 3):
             s3[s, pl.ds(16 * (d - 1), 16)] = f2[f, rows(16 * ((d3 + d) % 4), 16)].astype(BF)
             push(i, s3.at[s, pl.ds(16 * (d - 1), 16)], r3.at[i, pl.ds(16 * (d - 1), 16)], in3.at[i], to(d))
@@ -181,17 +169,13 @@
     def e6(i, k):
         (p1, _), (p2, to), _ = place(k)
         arrived(out.at[pl.ds(0, 48)], ag3.at[i])
-        gather(i, i * D + 256 * p1, 64, p2, to, fwd2)
-        others(i, i * D + 256 * p1, 64, p2, to, ag2)
-
-    def e7(i, k):
-        (p1, _), (p2, to), _ = place(k)
-        onward(i, i * D + 256 * p1, 64, p2, to, fwd2, ag2)
+        mine = out.at[rows(i * D + 256 * p1 + 64 * p2, 64)]
+        for d in (2, 1, 3):
+            push(i, mine, mine, ag2.at[i], to(d))
 
     def e8(i, k):
         (p1, to), _, _ = place(k)
-        for side in range(2):
-            arrived(out.at[pl.ds(0, 64)], ag2.at[i, side])
+        arrived(out.at[pl.ds(0, 192)], ag2.at[i])
         gather(i, i * D, 256, p1, to, fwd1)
 
     def e12(i, k):
@@ -207,7 +191,7 @@
             arrived(out.at[pl.ds(0, 256)], ag1.at[i, side])
         arrived(terms.at[pl.ds(0, 4 * 512 - 32)], send.at[i])
 
-    events = (e0, e1, e2, e3, e4, e5, e6, e7, e8, e9, e10, e11, e12)
+    events = (e0, e1, e2, None, e4, e5, e6, None, e8, e9, e10, e11, e12)
 
     g_start(0)
     for j in range(TOKENS // KB):
@@ -290,7 +274,7 @@
                 pltpu.VMEM((SLOTS, 2, 128, COLS), BF),
                 pltpu.VMEM((FSLOTS, 256, COLS), F32),
                 pltpu.VMEM((SLOTS, 192, COLS), BF),
-                pltpu.VMEM((ITEMS, 2, 96, COLS), BF),
+                pltpu.VMEM((ITEMS, 192, COLS), BF),
                 pltpu.VMEM((FSLOTS, 64, COLS), F32),
                 pltpu.VMEM((SLOTS, 48, COLS), BF),
                 pltpu.VMEM((ITEMS, 48, COLS), BF),
@@ -299,12 +283,10 @@
                 dma((SLOTS,)),
                 dma((ITEMS, 2)),
                 dma((ITEMS, 2)),
-                dma((ITEMS, 2)),
-                dma((ITEMS, 2)),
                 dma((ITEMS,)),
                 dma((ITEMS,)),
-                dma((ITEMS, 2)),
-                dma((ITEMS, 2)),
+                dma((ITEMS,)),
+                dma((ITEMS,)),
                 dma((ITEMS, 2)),
                 dma((ITEMS, 2)),
             ],

time: 145 us -> 142 us (0.979)
  Pallas kernels: 144 us -> 141 us
    pallas_call x1, Pallas kernels: 140 us -> 136 us  [step(): pl.pallas_call(kernel, out_shape=pltpu.VMEM((ITEMS * D, COLS), BF), in_sp...]
where the time goes in v3:
time: 142 us; the launch traced here: 141 us
  Pallas kernels  141 us (99%)
    pallas_call x1, Pallas kernels, step(): pl.pallas_call(kernel, out_shape=pltpu.VMEM((ITEMS * D, COLS), BF), in_sp...  136 us
    pallas_call x1, Pallas kernels, step(): pl.pallas_call(spread, out_shape=jax.ShapeDtypeStruct((2, D, FF), BF), in...  4.92 us

profile of v3, /device:TPU:0, one launch (start us, length us, event | category | flops | bytes accessed | tf_op | source)
XLA Modules:
  0.0 141.1 jit_solution(10459556423513986483)
XLA Ops:
  0.0 136.0 %shard_map.28.src = bf16[25600,256]{1,0:T(8,128)(2,1)S(1)} custom-call(bf16[1,2,4096,1024]{3,2,1,0:T(8,128)(2,1)} %a_hbm.1, bf16[1,2,4096,3200]{3,2,1,0:T(8,128)(2,1)} %g_hbm.1), custom_call_target="tpu_custom_call" | custom-call | tf_op jit(solution)/shard_map/pallas_call | solution.py:263
  136.0 4.9 %shard_map.29 = bf16[2,1024,3200]{2,1,0:T(8,128)(2,1)} custom-call(bf16[25600,256]{1,0:T(8,128)(2,1)S(1)} %shard_map.28.src), custom_call_target="tpu_custom_call" | custom-call | tf_op jit(solution)/shard_map/pallas_call | solution.py:296
